TPU v7x, 32 devices: a whole 2x2x4 slice. The times are simulated.
32 devices in a mesh: seq: 8 (over z, x), head: 4 (over y, core).
Axes of the slice: x: 2, y: 2, z: 4, core: 2. Of those that a mesh axis runs over, the one named last changes fastest.
Arguments:
- tokens: bfloat16 [8192, 2048], P('seq', 'head'), may hold values from -8 to 8
- w_query: bfloat16 [2048, 2048], P(None, 'head'), may hold values from -1 to 1, as said below
- w_key: bfloat16 [2048, 2048], P(None, 'head'), may hold values from -1 to 1, as said below
- w_value: bfloat16 [2048, 2048], P(None, 'head'), may hold values from -0.125 to 0.125
- w_out: bfloat16 [2048, 2048], P('head'), may hold values from -0.125 to 0.125
- mix_logit: float32 [8], P('head'), may hold values from -2 to 2
Outputs:
- layer_out: bfloat16 [8192, 2048], P('seq', 'head')
Inputs may be any that keep to these rules, and one draw needn't show every extreme that they name: `w_query`: entries of mean zero with a standard deviation of about 2048 ** -0.5. `w_key`: entries of mean zero with a standard deviation of about 2048 ** -0.5.
All inputs are finite; a program needn't handle non-finite values.
Results may differ from a plain program's by a relative error of at most 0.0065.
Values may be sent and summed in bfloat16 or wider, within the bound.
A program may use at most 128 MiB of HBM per device.

v0:
```python
import jax
import jax.numpy as jnp
from jax import lax
from jax.sharding import PartitionSpec as P


def entering(shard, axis, combine, identity):
    length, mine = (lax.axis_size(axis), lax.axis_index(axis))
    everything = jax.tree.map(lambda part: lax.all_gather(part, axis), shard)
    start = jax.tree.map(
        lambda part, zero: jnp.broadcast_to(jnp.asarray(zero, part.dtype), part.shape),
        shard,
        identity,
    )

    def hop(k, before):
        reached = k < mine
        new = combine(before, jax.tree.map(lambda part: part[k], everything))
        return jax.tree.map(lambda a, b: jnp.where(reached, a, b), new, before)

    return lax.fori_loop(0, length, hop, start)


def feature(values):
    return jax.nn.elu(values) + 1.0


def add_pairs(earlier, later):
    return (earlier[0] + later[0], earlier[1] + later[1])


def on_device(tokens, w_query, w_key, w_value, w_out, mix_logit):
    seg = tokens.shape[0]
    heads = mix_logit.shape[0]
    width = w_query.shape[1]
    hsize = width // heads
    empty = jnp.zeros((seg, width), jnp.float32)
    totals = (empty, empty, empty)
    piece = lax.all_gather(tokens, "head", axis=1, tiled=True)
    result = []
    for total, weight in zip(totals, (w_query, w_key, w_value)):
        result.append(jnp.dot(piece, weight, preferred_element_type=jnp.float32))
    query, keys, values = tuple(result)
    query = query.astype(jnp.bfloat16).reshape(seg, heads, hsize)
    keys = keys.astype(jnp.bfloat16).reshape(seg, heads, hsize)
    values = values.astype(jnp.bfloat16).reshape(seg, heads, hsize)
    fkey = feature(keys.astype(jnp.float32)).astype(jnp.bfloat16)
    mem_term = jnp.einsum("thd,the->hde", fkey, values, preferred_element_type=jnp.float32)
    norm_term = jnp.sum(fkey.astype(jnp.float32), axis=0)
    zeros_pair = (jnp.zeros_like(mem_term), jnp.zeros_like(norm_term))
    memory, normal = entering((mem_term, norm_term), "seq", add_pairs, zeros_pair)
    rows = lax.broadcasted_iota(jnp.int32, (seg, seg), 0)
    cols = lax.broadcasted_iota(jnp.int32, (seg, seg), 1)
    causal = cols <= rows
    scale = 1.0 / hsize**0.5
    scores = jnp.einsum("qhd,khd->hqk", query, keys, preferred_element_type=jnp.float32) * scale
    scores = jnp.where(causal[None], scores, -1e30)
    expo = jnp.exp(scores - jnp.max(scores, axis=2, keepdims=True))
    probs = (expo / jnp.sum(expo, axis=2, keepdims=True)).astype(jnp.bfloat16)
    local = jnp.einsum("hqk,khd->qhd", probs, values, preferred_element_type=jnp.float32)
    fquery = feature(query.astype(jnp.float32)).astype(jnp.bfloat16).astype(jnp.float32)
    numer = jnp.einsum("thd,hde->the", fquery, memory, precision=lax.Precision.HIGHEST)
    denom = jnp.einsum("thd,hd->th", fquery, normal, precision=lax.Precision.HIGHEST)
    readout = numer / jnp.maximum(denom, 1.0)[:, :, None]
    share = jax.nn.sigmoid(mix_logit)[None, :, None]
    mixed = (share * readout + (1.0 - share) * local).astype(jnp.bfloat16).reshape(seg, width)
    columns = lax.all_to_all(w_out, "head", split_axis=1, concat_axis=0, tiled=True)
    summed = jnp.dot(
        lax.all_gather(mixed, "head", axis=1, tiled=True),
        columns,
        preferred_element_type=jnp.float32,
    )
    return summed.astype(jnp.bfloat16)


def solution(mesh):
    placed = (
        P("seq", "head"),
        P(None, "head"),
        P(None, "head"),
        P(None, "head"),
        P("head", None),
        P("head"),
    )
    return jax.shard_map(
        on_device, mesh=mesh, in_specs=placed, out_specs=P("seq", "head"), check_vma=False
    )
```

profile of v0, /device:TPU:29, one launch (start us, length us, event | category | flops | bytes accessed | tf_op | source)
XLA Modules:
  0.0 221.5 jit_solution(13663326590009232278)
XLA Ops:
  6.5 0.0 copy-start
  6.5 0.0 all-gather.5.cloned.1.call-start
  6.5 0.7 all-gather.5.cloned.1.call-update
  7.3 0.0 all-gather.9.cloned.1.call-start
  7.3 36.5 %all-gather.5.cloned.1.call-done = bf16[1024,2048]{1,0:T(8,128)(2,1)} async-done(((bf16[1024,512]{1,0:T(8,128)(2,1)}), bf16[1024,2048]{1,0:T(8,128)(2,1)}) %all-gather.5.cloned.1.call-update) | async-done | bytes 4194320 | tf_op jit(solution)/shard_map/all_gather | solution.py:39
  43.8 0.0 copy-done
  43.8 6.3 %convert_reduce_fusion = (f32[512]{0:T(512)S(1)}, bf16[1024,512]{0,1:T(8,128)(2,1)}) fusion(bf16[1024,2048]{1,0:T(8,128)(2,1)} %all-gather.5.cloned.1.call-done, bf16[2048,512]{1,0:T(8,128)(2,1)S(1)} %copy-done), kind=kOutput, calls=%fused_computation.31 | convolution fusion | flops 2152201728 | bytes 7342080 | tf_op jit(solution)/shard_map/dot_general | solution.py:42
  50.1 2.3 %copy.33 = bf16[1024,2,256]{2,0,1:T(8,128)(2,1)} copy(bf16[1024,2,256]{0,2,1:T(8,128)(2,1)} %bitcast.52) | data formatting | bytes 2097152 | tf_op jit(solution)/shard_map/reshape | solution.py:45
  52.3 0.0 copy-start.2
  52.3 5.3 %convolution_convert_fusion.2 = bf16[1024,512]{0,1:T(8,128)(2,1)S(1)} fusion(bf16[1024,2048]{1,0:T(8,128)(2,1)} %all-gather.5.cloned.1.call-done, bf16[2048,512]{1,0:T(8,128)(2,1)} %param.11), kind=kOutput, calls=%fused_computation.34 | convolution fusion | flops 2148007936 | bytes 7340032 | tf_op jit(solution)/shard_map/dot_general | solution.py:42
  57.7 0.0 copy-start.4
  57.7 1.0 copy-done.4
  58.6 0.0 copy-done.2
  58.6 0.0 copy-start.3
  58.6 2.0 fusion.17
  60.7 0.0 all-gather.9.cloned.1.call-update
  60.7 0.0 all-gather.7.cloned.1.call-start
  60.8 1.3 iota_compare_fusion
  62.1 0.0 copy-done.3
  62.1 6.2 %convolution_convert_fusion.1 = bf16[1024,512]{0,1:T(8,128)(2,1)} fusion(bf16[1024,2048]{1,0:T(8,128)(2,1)} %all-gather.5.cloned.1.call-done, bf16[2048,512]{1,0:T(8,128)(2,1)} %param.9), kind=kOutput, calls=%fused_computation.33 | convolution fusion | flops 2148007936 | bytes 7340032 | tf_op jit(solution)/shard_map/dot_general | solution.py:42
  68.3 2.3 %copy.36 = bf16[1024,2,256]{2,0,1:T(8,128)(2,1)} copy(bf16[1024,2,256]{0,2,1:T(8,128)(2,1)} %bitcast.55) | data formatting | bytes 2097152 | tf_op jit(solution)/shard_map/reshape | solution.py:44
  70.6 19.6 %all_gather.22 = f32[8,2,256]{2,1,0:T(2,128)S(1)} all-gather(f32[1,2,256]{2,1,0:T(2,128)S(1)} %all_gather.21), channel_id=1, replica_groups=mesh['seq'=8,'head'=4] {'seq'}, dimensions={0}, use_global_device_ids=true | all-gather | bytes 18432 | tf_op jit(solution)/shard_map/all_gather | solution.py:9
  90.2 8.4 %fusion.36 = (f32[2,1024]{1,0:T(2,128)S(1)}, f32[2,1024,1024]{1,2,0:T(8,128)}) fusion(pred[1024,1024]{0,1:T(8,128)(4,1)} %iota_compare_fusion, bf16[1024,2,256]{0,2,1:T(8,128)(2,1)} %bitcast.56, bf16[1024,2,256]{0,2,1:T(8,128)(2,1)} %bitcast.53), kind=kOutput, calls=%fused_computation.54 | convolution fusion | flops 1082131456 | bytes 11542528 | tf_op jit(solution)/shard_map/sub | solution.py:58
  98.6 6.3 %fusion.4 = f32[2,256,1024]{2,1,0:T(8,128)} fusion(bf16[1024,2,256]{0,2,1:T(8,128)(2,1)} %bitcast.59, f32[2,1024,1024]{1,2,0:T(8,128)} %get-tuple-element.153, f32[2,1024]{1,0:T(2,128)S(1)} %get-tuple-element.152), kind=kOutput, calls=%fused_computation.16 | convolution fusion | flops 1077936128 | bytes 11542528 | tf_op jit(solution)/shard_map/hqk,khd->qhd/dot_general | solution.py:60
  105.0 27.9 %all-gather.9.cloned.1.call-done = f32[16,256,256]{2,1,0:T(8,128)} async-done(((f32[2,256,256]{2,1,0:T(8,128)}), f32[16,256,256]{2,1,0:T(8,128)}) %all-gather.9.cloned.1.call-update) | async-done | bytes 4194320 | tf_op jit(solution)/shard_map/all_gather | solution.py:9
  132.9 10.0 %while.16 = (s32[]{:T(128)}, f32[2,256,256]{2,1,0:T(8,128)S(1)}, f32[2,256]{1,0:T(2,128)S(1)}, s32[]{:T(128)}, f32[8,2,256,256]{3,2,1,0:T(8,128)}, /*index=5*/f32[8,2,256]{2,1,0:T(2,128)S(1)}, s32[]{:T(128)}, s32[]{:T(128)}) while((s32[]{:T(128)}, f32[2,256,256]{2,1,0:T(8,128)S(1)}, f32[2,256]{1,0:T(2,128)S(1)}, s32[]{:T(128)}, ...), condition=%wide.region_2.3_spmd.clone, body=%wide.region_1.2_spmd.clone.sunk | while | flops 394756 | bytes 1579131 | solution.py:21
  132.9 1.2 add_select_fusion.4
  134.1 1.2 add_select_fusion.4
  135.3 1.2 add_select_fusion.4
  136.6 1.2 add_select_fusion.4
  137.8 1.2 add_select_fusion.4
  139.1 1.2 add_select_fusion.4
  140.3 1.2 add_select_fusion.4
  141.6 1.2 add_select_fusion.4
  142.8 0.0 copy-start.1
  142.8 0.0 copy-start.5
  142.8 2.9 %fusion.23 = f32[2,1,1024]{2,1,0:T(1,128)S(1)} fusion(bf16[1024,2,256]{2,0,1:T(8,128)(2,1)} %copy.36, f32[2,256,1]{1,0,2:T(2,128)S(1)} %bitcast.57), kind=kOutput, calls=%fused_computation.40 | convolution fusion | flops 9437184 | bytes 1058816 | tf_op jit(solution)/shard_map/thd,hd->th/dot_general | solution.py:63
  145.8 0.0 copy-done.1
  145.8 0.0 copy-done.5
  145.8 3.8 %fusion.15 = bf16[1024,2,256]{0,2,1:T(8,128)(2,1)} fusion(f32[2,256,1024]{2,1,0:T(8,128)S(1)} %copy-done.5, f32[2,256,256]{2,1,0:T(8,128)S(1)} %get-tuple-element.115, f32[2]{0:T(128)S(1)} %get-tuple-element.150, f32[1024,2]{0,1:T(2,128)S(1)} %fusion.26, f32[2]{0:T(128)S(1)} %get-tuple-element.151, bf16[1024,2,256]{2,0,1:T(8,128)(2,1)S(1)} %copy-done.1), kind=kOutput, calls=%fused_computation.28 | convolution fusion | flops 1616379904 | bytes 4726800 | tf_op jit(solution)/shard_map/thd,hde->the/dot_general | solution.py:62
  149.6 0.0 all-gather.7.cloned.1.call-update
  149.6 4.0 %copy.41 = bf16[512,2048]{0,1:T(8,128)(2,1)} copy(bf16[512,2048]{1,0:T(8,128)(2,1)} %param.12) | data formatting | bytes 4194304 | tf_op args[4]
  153.6 51.0 %all_to_all.19 = bf16[512,4,512]{0,2,1:T(8,128)(2,1)} all-to-all(bf16[512,4,512]{0,2,1:T(8,128)(2,1)} %bitcast.49), channel_id=1, replica_groups=mesh['seq'=8,'head'=4] {'head'}, dimensions={1} | all-to-all | bytes 4194304 | tf_op jit(solution)/shard_map/all_to_all | solution.py:67
  204.6 4.2 %copy.42 = bf16[4,512,512]{2,1,0:T(8,128)(2,1)} copy(bf16[4,512,512]{1,2,0:T(8,128)(2,1)} %bitcast.48) | data formatting | bytes 4194304 | tf_op jit(solution)/shard_map/all_to_all | solution.py:67
  208.8 0.0 all-gather.7.cloned.1.call-done
  208.8 6.2 %convolution_convert_fusion = bf16[1024,512]{1,0:T(8,128)(2,1)} fusion(bf16[1024,2048]{0,1:T(8,128)(2,1)} %all-gather.7.cloned.1.call-done, bf16[2048,512]{1,0:T(8,128)(2,1)} %bitcast.50), kind=kOutput, calls=%fused_computation.32 | convolution fusion | flops 2148007936 | bytes 7340032 | tf_op jit(solution)/shard_map/dot_general | solution.py:68
  (13 shorter events, 0.2 us)
Async XLA Ops:
  6.5 37.3 %copy-start = (bf16[2048,512]{1,0:T(8,128)(2,1)S(1)}, bf16[2048,512]{1,0:T(8,128)(2,1)}, u32[]{:S(2)}) copy-start(bf16[2048,512]{1,0:T(8,128)(2,1)} %param.10) | copy-start | bytes 6291460
  6.5 37.3 %all-gather.5.cloned.1.call-start = ((), (), s32[]{:S(2)}) async-start(), calls=%async_computation.1 | async-start | bytes 5242880 | tf_op jit(solution)/shard_map/all_gather | solution.py:39
  7.3 125.6 %all-gather.9.cloned.1.call-start = ((), (), s32[]{:S(2)}) async-start(), calls=%async_computation.3 | async-start | bytes 4718592 | tf_op jit(solution)/shard_map/all_gather | solution.py:9
  52.3 6.3 %copy-start.2 = (bf16[1024,2,256]{2,0,1:T(8,128)(2,1)S(1)}, bf16[1024,2,256]{2,0,1:T(8,128)(2,1)}, u32[]{:S(2)}) copy-start(bf16[1024,2,256]{2,0,1:T(8,128)(2,1)} %copy.33) | copy-start | bytes 3145732
  57.7 1.0 copy-start.4
  58.6 3.4 %copy-start.3 = (f32[2]{0:T(128)S(1)}, f32[2]{0:T(128)}, u32[]{:S(2)}) copy-start(f32[2]{0:T(128)} %param.13) | copy-start | bytes 28
  60.7 148.1 %all-gather.7.cloned.1.call-start = ((), (), s32[]{:S(2)}) async-start(), calls=%async_computation.2 | async-start | bytes 5242880 | tf_op jit(solution)/shard_map/all_gather | solution.py:69
  142.8 3.0 %copy-start.1 = (bf16[1024,2,256]{2,0,1:T(8,128)(2,1)S(1)}, bf16[1024,2,256]{2,0,1:T(8,128)(2,1)}, u32[]{:S(2)}) copy-start(bf16[1024,2,256]{2,0,1:T(8,128)(2,1)} %copy.36) | copy-start | bytes 3145732
  142.8 3.0 %copy-start.5 = (f32[2,256,1024]{2,1,0:T(8,128)S(1)}, f32[2,256,1024]{2,1,0:T(8,128)}, u32[]{:S(2)}) copy-start(f32[2,256,1024]{2,1,0:T(8,128)} %fusion.4) | copy-start | bytes 6291460
Sparse Core Ops, SparseCore 0:
  8.9 34.8 all-gather.4
  60.8 71.9 all-gather.8
  149.7 56.0 all-gather.6
where the time goes:
time: 225 us; the launch traced here: 222 us
  blocking collectives  70.6 us (31%)
  waiting for transfers between devices  65.1 us (29%)
  matrix products  47.5 us (21%)
  local copies, waits for them, and re-layouts  13.8 us (6%)
  between operations  13.2 us (6%)
  other arithmetic  11.1 us (5%)
    all_to_all x1, blocking collectives, on_device(): lax.all_to_all(w_out, 'head', split_axis=1, concat_axis=0, tiled=True)  51 us
    all_gather x1, waiting for transfers between devices, on_device(): piece = lax.all_gather(tokens, 'head', axis=1, tiled=True)  36.5 us
    all_gather x1, waiting for transfers between devices, entering(): everything = jax.tree.map(lambda part: lax.all_gather(part, axis), shard)  27.9 us
    all_gather x1, blocking collectives, entering(): everything = jax.tree.map(lambda part: lax.all_gather(part, axis), shard)  19.6 us
    dot_general x3, matrix products, on_device(): result.append(jnp.dot(piece, weight, preferred_element_type=jnp.float32))  17.8 us
    select_n x16, other arithmetic, hop(): return jax.tree.map(lambda a, b: jnp.where(reached, a, b), new, before)  9.76 us
    sub x1, matrix products, on_device(): expo = jnp.exp(scores - jnp.max(scores, axis=2, keepdims=True))  8.37 us
    dot_general x1, matrix products, on_device(): jnp.einsum('hqk,khd->qhd', probs, values, preferred_element_type=jnp.floa...  6.33 us
  transfers between devices with their start and end apart: 3, of which 2 were waited for; matrix products, arithmetic and copies ran while one was open for 15% of the time, Pallas kernels for 0%

commit v1 on v0

v1 whole, which is shorter than its diff:
```python
import functools

import jax
import jax.numpy as jnp
from jax import lax
from jax.experimental import pallas as pl
from jax.experimental.pallas import tpu as pltpu
from jax.sharding import PartitionSpec as P

MESH = pl.DeviceIdType.MESH
CHUNKS = 4
PAD = 16
BF16 = jnp.bfloat16
F32 = jnp.float32


def feature(values):
    return jnp.where(values > 0.0, values + 1.0, jnp.exp(jnp.minimum(values, 0.0)))


def matmul(a, b):
    return jnp.dot(a, b, preferred_element_type=F32)


def kernel(
    groups, tok, wq, wk, wv, wo, logit, out,
    x, w, wos, q, k, v, loc, mix, psend, precv, outv, term, s1send, s1recv, s2send, s2recv, s3send, memory,
    tok_sem, w_sem, wo_sem, wos_s, wos_r, sib_s, sib_r, cross_s, cross_r, far_s, far_r,
    e1_s, e1_r, e2_s, e2_r, e3_s, e3_r, mix_s, mix_r, p_s, p_r, out_sem,
):
    seg, feats = tok.shape
    width = wq.shape[1]
    heads = logit.shape[0]
    hsize = width // heads
    half = heads // 2
    rows_of = seg // CHUNKS
    here, sq = lax.axis_index("head"), lax.axis_index("seq")
    sib = here + 1 - 2 * lax.rem(here, 2)
    cross = lax.rem(here + 2, 4)
    far = lax.rem(sib + 2, 4)
    b, a = lax.rem(sq, 2), lax.div(sq, 2)
    pair = sq + 1 - 2 * b

    def rows(i):
        return pl.ds(i * rows_of, rows_of)

    def block(index, size):
        return pl.ds(pl.multiple_of(index * size, size), size)

    def remote(src, dst, send, recv, head=None, seq=None):
        target = (sq if seq is None else seq, here if head is None else head)
        return pltpu.make_async_remote_copy(
            src_ref=src, dst_ref=dst, send_sem=send, recv_sem=recv, device_id=target, device_id_type=MESH
        )

    own_tok = [
        pltpu.make_async_copy(tok.at[rows(i), :], x.at[rows(i), pl.ds(0, feats)], tok_sem.at[i]) for i in range(CHUNKS)
    ]
    own_tok[0].start()
    order = (here, sib, cross, far)
    weights = []
    for slot, device in enumerate(order):
        for t, weight in enumerate((wq, wk, wv)):
            copy = pltpu.make_async_copy(
                weight.at[block(device, feats), :], w.at[t, pl.ds(slot * feats, feats), :], w_sem.at[t, slot]
            )
            copy.start()
            weights.append(copy)
    for copy in own_tok[1:]:
        copy.start()
    own_wo = [
        pltpu.make_async_copy(
            wo.at[:, block(device, feats)], wos.at[pl.ds(0, width), pl.ds(j * feats, feats)], wo_sem.at[j]
        )
        for j, device in enumerate((here, cross))
    ]
    for copy in own_wo:
        copy.start()

    barrier = pltpu.get_barrier_semaphore()
    partners = [(sq, sib), (sq, cross), (pair, here)]
    for d in range(1, groups):
        partners.append((2 * lax.rem(a + d, groups) + b, here))
    for partner in partners:
        pl.semaphore_signal(barrier, inc=1, device_id=partner, device_id_type=MESH)
    pl.semaphore_wait(barrier, len(partners))

    to_cross = [
        remote(tok.at[rows(i), :], x.at[rows(i), pl.ds(2 * feats, feats)], cross_s.at[i], cross_r.at[i], head=cross)
        for i in range(CHUNKS)
    ]
    to_sib = [
        remote(tok.at[rows(i), :], x.at[rows(i), pl.ds(feats, feats)], sib_s.at[i], sib_r.at[i], head=sib)
        for i in range(CHUNKS)
    ]
    forward = [
        remote(
            x.at[rows(i), pl.ds(2 * feats, feats)],
            x.at[rows(i), pl.ds(3 * feats, feats)],
            far_s.at[i],
            far_r.at[i],
            head=sib,
        )
        for i in range(CHUNKS)
    ]
    for i in range(CHUNKS):
        to_cross[i].start()
        to_sib[i].start()
    to_wos = [
        remote(
            wo.at[:, block(device, feats)],
            wos.at[pl.ds(width, width), pl.ds(j * feats, feats)],
            wos_s.at[j],
            wos_r.at[j],
            head=sib,
        )
        for j, device in enumerate((sib, far))
    ]
    for copy in to_wos:
        copy.start()

    term[...] = jnp.zeros_like(term)
    scale = 1.0 / hsize**0.5

    def attention(i, h):
        cols = pl.ds(h * hsize, hsize)
        query = q[rows(i), cols]
        spot = lax.broadcasted_iota(jnp.int32, (rows_of, rows_of), 0)
        causal = lax.broadcasted_iota(jnp.int32, (rows_of, rows_of), 1) <= spot

        def scores_of(span):
            return lax.dot_general(query, k[span, cols], (((1,), (1,)), ((), ())), preferred_element_type=F32) * scale

        last = jnp.where(causal, scores_of(rows(i)), -1e30)
        top = jnp.max(last, axis=1, keepdims=True)
        if i:
            before = pl.ds(0, i * rows_of)
            first = scores_of(before)
            top = jnp.maximum(top, jnp.max(first, axis=1, keepdims=True))
        expo = jnp.exp(last - top)
        total = jnp.sum(expo, axis=1, keepdims=True)
        value = matmul(expo.astype(BF16), v[rows(i), cols])
        if i:
            expo = jnp.exp(first - top)
            total = total + jnp.sum(expo, axis=1, keepdims=True)
            value = value + matmul(expo.astype(BF16), v[before, cols])
        loc[rows(i), cols] = value / total

    for i in range(CHUNKS):
        to_cross[i].wait_recv()
        forward[i].start()
        if i:
            for h in range(heads):
                attention(i - 1, h)
        own_tok[i].wait()
        to_sib[i].wait_recv()
        if i == 0:
            for copy in weights:
                copy.wait()
        forward[i].wait_recv()
        for t, target in ((1, k), (2, v)):
            target[rows(i), :] = matmul(x[rows(i), :], w[t]).astype(BF16)
        for h in range(heads):
            cols = pl.ds(h * hsize, hsize)
            fkey = feature(k[rows(i), cols].astype(F32)).astype(BF16)
            term[h, pl.ds(0, hsize), :] += lax.dot_general(
                fkey, v[rows(i), cols], (((0,), (0,)), ((), ())), preferred_element_type=F32
            )
            term[h, pl.ds(hsize, PAD), :] += jnp.broadcast_to(
                jnp.sum(fkey.astype(F32), axis=0, keepdims=True), (PAD, hsize)
            )
        if i < CHUNKS - 1:
            q[rows(i), :] = matmul(x[rows(i), :], w[0]).astype(BF16)

    mine, other = pl.ds(b * half, half), pl.ds((1 - b) * half, half)
    s1send[...] = term[other].astype(BF16)
    swap = remote(s1send, s1recv, e1_s, e1_r, seq=pair)
    swap.start()
    q[rows(CHUNKS - 1), :] = matmul(x[rows(CHUNKS - 1), :], w[0]).astype(BF16)
    swap.wait_recv()
    s2send[...] = (term[mine] + s1recv[...].astype(F32)).astype(BF16)

    def later(d):
        return remote(s2send, s2recv.at[a], e2_s.at[d], e2_r.at[a], seq=sq + 2 * d)

    for d in range(1, groups):

        @pl.when(a + d < groups)
        def _(d=d):
            later(d).start()

    for h in range(heads):
        attention(CHUNKS - 1, h)

    s3 = jnp.where(b == 0, term[mine], 0.0)
    term[other] = jnp.where(b == 1, s1recv[...].astype(F32), 0.0)
    term[mine] = s3
    for g in range(groups - 1):

        @pl.when(g < a)
        def _(g=g):
            remote(s2send, s2recv.at[g], e2_s.at[0], e2_r.at[g], seq=pair).wait_recv()
            got = s2recv[g].astype(F32)
            term[mine] += got
            term[other] += got

    s3send[...] = term[mine].astype(BF16)
    back = remote(s3send, memory.at[mine], e3_s, e3_r, seq=pair)
    back.start()
    memory[mine] = term[other].astype(BF16)

    to_mix = [
        remote(
            mix.at[rows(i), pl.ds(0, width)], mix.at[rows(i), pl.ds(width, width)], mix_s.at[i], mix_r.at[i], head=sib
        )
        for i in range(CHUNKS)
    ]
    to_p = [remote(psend.at[rows(i), :], precv.at[rows(i), :], p_s.at[i], p_r.at[i], head=cross) for i in range(CHUNKS)]
    to_out = [pltpu.make_async_copy(outv.at[rows(i), :], out.at[rows(i), :], out_sem.at[i]) for i in range(CHUNKS)]

    def readout(i):
        for h in range(heads):
            cols = pl.ds(h * hsize, hsize)
            share = jax.nn.sigmoid(jnp.full((1, hsize), logit[h], F32))
            fquery = feature(q[rows(i), cols].astype(F32)).astype(BF16)
            numer = matmul(fquery, memory[h, pl.ds(0, hsize), :])
            normal = memory[h, pl.ds(hsize, PAD), :].astype(F32)[0:1]
            denom = jnp.sum(fquery.astype(F32) * normal, axis=1, keepdims=True)
            read = numer / jnp.maximum(denom, 1.0)
            mix[rows(i), cols] = (share * read + (1.0 - share) * loc[rows(i), cols]).astype(BF16)
        to_mix[i].start()

    def partial(i):
        to_mix[i].wait_recv()
        if i == 0:
            for copy in own_wo:
                copy.wait()
            for copy in to_wos:
                copy.wait_recv()
        psend[rows(i), :] = matmul(mix[rows(i), :], wos[:, pl.ds(feats, feats)]).astype(BF16)
        to_p[i].start()

    back.wait_recv()
    readout(0)
    for i in range(1, CHUNKS):
        readout(i)
        partial(i - 1)
    partial(CHUNKS - 1)
    for i in range(CHUNKS):
        own = matmul(mix[rows(i), :], wos[:, pl.ds(0, feats)])
        to_p[i].wait_recv()
        outv[rows(i), :] = (own + precv[rows(i), :].astype(F32)).astype(BF16)
        to_out[i].start()

    for i in range(CHUNKS):
        for copies in (to_cross, to_sib, forward, to_mix, to_p):
            copies[i].wait_send()
    for copy in to_wos + [swap, back]:
        copy.wait_send()
    for d in range(1, groups):

        @pl.when(a + d < groups)
        def _(d=d):
            later(d).wait_send()

    for copy in to_out:
        copy.wait()


def on_device(groups, tokens, w_query, w_key, w_value, w_out, mix_logit):
    seg, feats = tokens.shape
    depth, width = w_query.shape
    heads = mix_logit.shape[0]
    hsize = width // heads
    half = heads // 2
    dma = pltpu.SemaphoreType.DMA
    piece = (half, hsize + PAD, hsize)
    anywhere = pl.BlockSpec(memory_space=pl.ANY)
    return pl.pallas_call(
        functools.partial(kernel, groups),
        out_shape=jax.ShapeDtypeStruct((seg, feats), BF16),
        in_specs=[anywhere] * 5 + [pl.BlockSpec(memory_space=pltpu.SMEM)],
        out_specs=anywhere,
        scratch_shapes=[
            pltpu.VMEM((seg, depth), BF16),
            pltpu.VMEM((3, depth, width), BF16),
            pltpu.VMEM((2 * width, 2 * feats), BF16),
            pltpu.VMEM((seg, width), BF16),
            pltpu.VMEM((seg, width), BF16),
            pltpu.VMEM((seg, width), BF16),
            pltpu.VMEM((seg, width), F32),
            pltpu.VMEM((seg, 2 * width), BF16),
            pltpu.VMEM((seg, feats), BF16),
            pltpu.VMEM((seg, feats), BF16),
            pltpu.VMEM((seg, feats), BF16),
            pltpu.VMEM((heads, hsize + PAD, hsize), F32),
            pltpu.VMEM(piece, BF16),
            pltpu.VMEM(piece, BF16),
            pltpu.VMEM(piece, BF16),
            pltpu.VMEM((groups,) + piece, BF16),
            pltpu.VMEM(piece, BF16),
            pltpu.VMEM((heads, hsize + PAD, hsize), BF16),
            dma((CHUNKS,)),
            dma((3, 4)),
            dma((2,)),
            dma((2,)),
            dma((2,)),
        ]
        + [dma((CHUNKS,))] * 6
        + [dma, dma, dma((groups,)), dma((groups,)), dma, dma]
        + [dma((CHUNKS,))] * 5,
        compiler_params=pltpu.CompilerParams(collective_id=0, has_side_effects=True, vmem_limit_bytes=64000000),
    )(tokens, w_query, w_key, w_value, w_out, mix_logit)


def solution(mesh):
    placed = (
        P("seq", "head"),
        P(None, "head"),
        P(None, "head"),
        P(None, "head"),
        P("head", None),
        P("head"),
    )
    return jax.shard_map(
        functools.partial(on_device, mesh.shape["seq"] // 2),
        mesh=mesh,
        in_specs=placed,
        out_specs=P("seq", "head"),
        check_vma=False,
    )
```

time: 225 us -> 83.5 us (0.37); the launches traced: 222 us -> 83.4 us
  Pallas kernels: 0 us -> 81.1 us
  blocking collectives: 70.6 us -> 0 us
  waiting for transfers between devices: 65.1 us -> 0 us
  matrix products: 47.5 us -> 0 us
  between operations: 13.2 us -> 0.01 us
  local copies, waits for them, and re-layouts: 13.8 us -> 2.26 us
  other arithmetic: 11.1 us -> 0 us
    pallas_call x0 -> x1, Pallas kernels: none -> 81.1 us  [on_device(): pl.pallas_call(functools.partial(kernel, groups), out_shape=jax.ShapeDtyp...]
    all_gather x3 -> x0, waiting for transfers between devices: 64.4 us -> none  [the longest x1 36.5 us: on_device(): piece = lax.all_gather(tokens, 'head', axis=1, tiled=True)]
    all_to_all x1 -> x0, blocking collectives: 51 us -> none  [on_device(): lax.all_to_all(w_out, 'head', split_axis=1, concat_axis=0, tiled=True)]
    dot_general x8 -> x0, matrix products: 39.1 us -> none  [the longest x3 17.8 us: on_device(): result.append(jnp.dot(piece, weight, preferred_element_type=jnp.float32))]
    all_gather x1 -> x0, blocking collectives: 19.6 us -> none  [entering(): everything = jax.tree.map(lambda part: lax.all_gather(part, axis), shard)]
    select_n x16 -> x0, other arithmetic: 9.76 us -> none  [hop(): return jax.tree.map(lambda a, b: jnp.where(reached, a, b), new, before)]
    sub x1 -> x0, matrix products: 8.37 us -> none  [on_device(): expo = jnp.exp(scores - jnp.max(scores, axis=2, keepdims=True))]
    reshape x2 -> x0, local copies, waits for them, and re-layouts: 4.55 us -> none  [the longest x1 2.29 us: on_device(): query = query.astype(jnp.bfloat16).reshape(seg, heads, hsize)]
  transfers between devices with their start and end apart: 3 -> 0, of which waited for: 2 -> 0; matrix products, arithmetic and copies ran while one was open for 15% -> 0% of each run, Pallas kernels for 0% -> 0%
where the time goes in v1:
time: 83.5 us; the launch traced here: 83.4 us
  Pallas kernels  81.1 us (97%)
  local copies, waits for them, and re-layouts  2.26 us (3%)
    pallas_call x1, Pallas kernels, on_device(): pl.pallas_call(functools.partial(kernel, groups), out_shape=jax.ShapeDtyp...  81.1 us
    unnamed x1, local copies, waits for them, and re-layouts  2.26 us

profile of v1, /device:TPU:29, one launch (start us, length us, event | category | flops | bytes accessed | tf_op | source)
XLA Modules:
  0.0 83.4 jit_solution(11091559482826036742)
XLA Ops:
  0.0 81.1 %shard_map.64 = bf16[1024,512]{1,0:T(8,128)(2,1)} custom-call(bf16[1024,512]{1,0:T(8,128)(2,1)} %tok.1, bf16[2048,512]{1,0:T(8,128)(2,1)} %wq.1, bf16[2048,512]{1,0:T(8,128)(2,1)} %wk.1, bf16[2048,512]{1,0:T(8,128)(2,1)} %wv.1, bf16[512,2048]{1,0:T(8,128)(2,1)} %wo.1, f32[2]{0:T(128)} %logit.1), custom_call_target="tpu_custom_call" | custom-call | tf_op jit(solution)/shard_map/pallas_call | solution.py:279
  81.1 2.3 %copy.8 = bf16[1024,512]{1,0:T(8,128)(2,1)} copy(bf16[1024,512]{1,0:T(8,128)(2,1)} %shard_map.64) | data formatting | bytes 2097152

commit v2 on v1

--- a/solution.py
+++ b/solution.py
@@ -8,7 +8,8 @@
 from jax.sharding import PartitionSpec as P
 
 MESH = pl.DeviceIdType.MESH
-CHUNKS = 4
+CHUNKS = 8
+PIECES = 8
 PAD = 16
 BF16 = jnp.bfloat16
 F32 = jnp.float32
@@ -79,7 +80,7 @@
 
     barrier = pltpu.get_barrier_semaphore()
     partners = [(sq, sib), (sq, cross), (pair, here)]
-    for d in range(1, groups):
+    for d in (1, groups - 1):
         partners.append((2 * lax.rem(a + d, groups) + b, here))
     for partner in partners:
         pl.semaphore_signal(barrier, inc=1, device_id=partner, device_id_type=MESH)
@@ -173,41 +174,51 @@
             q[rows(i), :] = matmul(x[rows(i), :], w[0]).astype(BF16)
 
     mine, other = pl.ds(b * half, half), pl.ds((1 - b) * half, half)
-    s1send[...] = term[other].astype(BF16)
-    swap = remote(s1send, s1recv, e1_s, e1_r, seq=pair)
-    swap.start()
+    step = hsize // PIECES
+    spans = [pl.ds(p * step, step + (PAD if p == PIECES - 1 else 0)) for p in range(PIECES)]
+    swap = [
+        remote(s1send.at[:, span], s1recv.at[:, span], e1_s.at[p], e1_r.at[p], seq=pair)
+        for p, span in enumerate(spans)
+    ]
+    chain = [
+        remote(s2send.at[:, span], s2recv.at[:, span], e2_s.at[p], e2_r.at[p], seq=sq + 2)
+        for p, span in enumerate(spans)
+    ]
+    back = [
+        remote(s3send.at[:, span], memory.at[mine, span], e3_s.at[p], e3_r.at[p], seq=pair)
+        for p, span in enumerate(spans)
+    ]
+    for p, span in enumerate(spans):
+        s1send[:, span] = term[other, span].astype(BF16)
+        swap[p].start()
+
+    @pl.when(a == 0)
+    def _():
+        s2recv[...] = jnp.zeros_like(s2recv)
+
     q[rows(CHUNKS - 1), :] = matmul(x[rows(CHUNKS - 1), :], w[0]).astype(BF16)
-    swap.wait_recv()
-    s2send[...] = (term[mine] + s1recv[...].astype(F32)).astype(BF16)
-
-    def later(d):
-        return remote(s2send, s2recv.at[a], e2_s.at[d], e2_r.at[a], seq=sq + 2 * d)
-
-    for d in range(1, groups):
-
-        @pl.when(a + d < groups)
-        def _(d=d):
-            later(d).start()
+    for p, span in enumerate(spans):
+        swap[p].wait_recv()
+
+        @pl.when(a > 0)
+        def _(p=p):
+            chain[p].wait_recv()
+
+        own = term[mine, span]
+        paired = s1recv[:, span].astype(F32)
+        before = s2recv[:, span].astype(F32)
+
+        @pl.when(a < groups - 1)
+        def _(p=p, span=span, total=before + own + paired):
+            s2send[:, span] = total.astype(BF16)
+            chain[p].start()
+
+        s3send[:, span] = (before + jnp.where(b == 0, own, 0.0)).astype(BF16)
+        back[p].start()
+        memory[mine, span] = (before + jnp.where(b == 1, paired, 0.0)).astype(BF16)
 
     for h in range(heads):
         attention(CHUNKS - 1, h)
-
-    s3 = jnp.where(b == 0, term[mine], 0.0)
-    term[other] = jnp.where(b == 1, s1recv[...].astype(F32), 0.0)
-    term[mine] = s3
-    for g in range(groups - 1):
-
-        @pl.when(g < a)
-        def _(g=g):
-            remote(s2send, s2recv.at[g], e2_s.at[0], e2_r.at[g], seq=pair).wait_recv()
-            got = s2recv[g].astype(F32)
-            term[mine] += got
-            term[other] += got
-
-    s3send[...] = term[mine].astype(BF16)
-    back = remote(s3send, memory.at[mine], e3_s, e3_r, seq=pair)
-    back.start()
-    memory[mine] = term[other].astype(BF16)
 
     to_mix = [
         remote(
@@ -240,7 +251,8 @@
         psend[rows(i), :] = matmul(mix[rows(i), :], wos[:, pl.ds(feats, feats)]).astype(BF16)
         to_p[i].start()
 
-    back.wait_recv()
+    for copy in back:
+        copy.wait_recv()
     readout(0)
     for i in range(1, CHUNKS):
         readout(i)
@@ -255,13 +267,12 @@
     for i in range(CHUNKS):
         for copies in (to_cross, to_sib, forward, to_mix, to_p):
             copies[i].wait_send()
-    for copy in to_wos + [swap, back]:
+    for copy in to_wos + swap + back:
         copy.wait_send()
-    for d in range(1, groups):
-
-        @pl.when(a + d < groups)
-        def _(d=d):
-            later(d).wait_send()
+    @pl.when(a < groups - 1)
+    def _():
+        for copy in chain:
+            copy.wait_send()
 
     for copy in to_out:
         copy.wait()
@@ -297,7 +308,7 @@
             pltpu.VMEM(piece, BF16),
             pltpu.VMEM(piece, BF16),
             pltpu.VMEM(piece, BF16),
-            pltpu.VMEM((groups,) + piece, BF16),
+            pltpu.VMEM(piece, BF16),
             pltpu.VMEM(piece, BF16),
             pltpu.VMEM((heads, hsize + PAD, hsize), BF16),
             dma((CHUNKS,)),
@@ -307,7 +318,7 @@
             dma((2,)),
         ]
         + [dma((CHUNKS,))] * 6
-        + [dma, dma, dma((groups,)), dma((groups,)), dma, dma]
+        + [dma((PIECES,))] * 6
         + [dma((CHUNKS,))] * 5,
         compiler_params=pltpu.CompilerParams(collective_id=0, has_side_effects=True, vmem_limit_bytes=64000000),
     )(tokens, w_query, w_key, w_value, w_out, mix_logit)

time: 83.5 us -> 76.9 us (0.921)
  Pallas kernels: 81.1 us -> 74.5 us
    pallas_call x1, Pallas kernels: 81.1 us -> 74.5 us  [on_device(): pl.pallas_call(functools.partial(kernel, groups), out_shape=jax.ShapeDtyp...]
where the time goes in v2:
time: 76.9 us; the launch traced here: 76.7 us
  Pallas kernels  74.5 us (97%)
  local copies, waits for them, and re-layouts  2.26 us (3%)
    pallas_call x1, Pallas kernels, on_device(): pl.pallas_call(functools.partial(kernel, groups), out_shape=jax.ShapeDtyp...  74.5 us
    unnamed x1, local copies, waits for them, and re-layouts  2.26 us

profile of v2, /device:TPU:29, one launch (start us, length us, event | category | flops | bytes accessed | tf_op | source)
XLA Modules:
  0.0 76.7 jit_solution(2754742943539398919)
XLA Ops:
  0.0 74.5 %shard_map.64 = bf16[1024,512]{1,0:T(8,128)(2,1)} custom-call(bf16[1024,512]{1,0:T(8,128)(2,1)} %tok.1, bf16[2048,512]{1,0:T(8,128)(2,1)} %wq.1, bf16[2048,512]{1,0:T(8,128)(2,1)} %wk.1, bf16[2048,512]{1,0:T(8,128)(2,1)} %wv.1, bf16[512,2048]{1,0:T(8,128)(2,1)} %wo.1, f32[2]{0:T(128)} %logit.1), custom_call_target="tpu_custom_call" | custom-call | tf_op jit(solution)/shard_map/pallas_call | solution.py:290
  74.5 2.3 %copy.8 = bf16[1024,512]{1,0:T(8,128)(2,1)} copy(bf16[1024,512]{1,0:T(8,128)(2,1)} %shard_map.64) | data formatting | bytes 2097152
